TPU v7x, 128 devices: a whole 4x4x4 slice. The times are simulated.
128 devices in a mesh: dp: 8 (over x, core), tensor: 16 (over z, y).
Axes of the slice: x: 4, y: 4, z: 4, core: 2. Of those that a mesh axis runs over, the one named last changes fastest.
Arguments:
- activations: bfloat16 [4096, 28672], P('dp', 'tensor'), parts along dimension 0, may hold values from -6 to 6
- down_weight: bfloat16 [28672, 6144], P('tensor'), may hold values from -0.046875 to 0.046875
Outputs:
- projected: bfloat16 [4096, 6144], P(('dp', 'tensor')), parts along dimension 0
There are 8 independent parts, one for each index of `dp`. A program takes and returns all parts, laid end to end along the dimension named above; an argument that names none is the same for every part. Nothing has to cross between parts.
All inputs are finite; a program needn't handle non-finite values.
Results may differ from a plain program's by a relative error of at most 0.015.
Values may be sent and summed in bfloat16 or wider, within the bound.
A program may use at most 128 MiB of HBM per device.

v0:
```python
import math

import jax
import jax.numpy as jnp
import numpy as np
from jax import lax
from jax.sharding import PartitionSpec as P


def paley_matrix():
    modulus = 13
    residues = set((value * value % modulus for value in range(1, modulus)))
    jacobsthal = np.array(
        [
            [
                (
                    0.0
                    if row_at == col_at
                    else 1.0 if (col_at - row_at) % modulus in residues else -1.0
                )
                for col_at in range(modulus)
            ]
            for row_at in range(modulus)
        ]
    )
    confer = np.zeros((14, 14))
    confer[0, 1:] = 1.0
    confer[1:, 0] = 1.0
    confer[1:, 1:] = jacobsthal
    return np.kron(confer, np.array([[1.0, 1.0], [1.0, -1.0]])) + np.kron(
        np.eye(14), np.array([[1.0, -1.0], [-1.0, -1.0]])
    )


def sylvester(order):
    matrix = np.ones((1, 1))
    while matrix.shape[0] < order:
        matrix = np.kron(matrix, np.array([[1.0, 1.0], [1.0, -1.0]]))
    return matrix


def quantize(rotated, largest):
    token_scale = jnp.maximum(largest, 1.0)
    levels = 7.0 * rotated / token_scale
    snapped = levels - jnp.sin(2.0 * math.pi * levels) / (2.0 * math.pi)
    return (snapped * token_scale / 7.0).astype(jnp.bfloat16)


def shards(activations, down_weight):
    count_rows, shard_width = activations.shape
    groups = lax.axis_size("tensor")
    local_order = shard_width // 28
    rotation = jnp.asarray(np.kron(sylvester(local_order), paley_matrix()), jnp.bfloat16)
    mixed_rows = jnp.dot(activations, rotation, preferred_element_type=jnp.float32)
    normal_scale = 1.0 / math.sqrt(shard_width * groups)
    cross_table = jnp.asarray(sylvester(groups), jnp.float32)
    blocks = mixed_rows.reshape(groups, count_rows // groups, shard_width)
    rotated = (
        jnp.einsum(
            "ea,etf->atf",
            cross_table,
            lax.all_to_all(blocks, "tensor", split_axis=0, concat_axis=0, tiled=True),
        )
        * normal_scale
    )
    largest = jnp.max(jnp.abs(rotated), axis=(0, 2), keepdims=True)
    returned = lax.all_to_all(
        quantize(rotated, largest), "tensor", split_axis=0, concat_axis=0, tiled=True
    )
    dequant = returned.reshape(count_rows, shard_width)
    return lax.psum_scatter(
        jnp.dot(dequant, down_weight, preferred_element_type=jnp.float32).astype(jnp.bfloat16),
        "tensor",
        scatter_dimension=0,
        tiled=True,
    )


def solution(mesh):
    placed = (P("dp", "tensor"), P("tensor", None))
    return jax.shard_map(
        shards, mesh=mesh, in_specs=placed, out_specs=P(("dp", "tensor"), None), check_vma=False
    )
```

profile of v0, /device:TPU:0, one launch (start us, length us, event | category | flops | bytes accessed | tf_op | source)
XLA Modules:
  0.0 195.7 jit_solution(14328329271352309366)
XLA Ops:
  6.5 0.0 copy-start
  6.5 0.0 reduce-scatter.2.cloned.1.call-start
  6.5 1.5 copy-done
  8.0 6.3 %fusion.7 = bf16[1792,512]{0,1:T(8,128)(2,1)S(1)} fusion(bf16[512,1792]{1,0:T(8,128)(2,1)S(1)} %copy-done, bf16[1792,1792]{1,0:T(8,128)(2,1)} %constant.19.clone), kind=kOutput, calls=%fused_computation.12 | convolution fusion | flops 3288334336 | bytes 10092544 | tf_op jit(solution)/shard_map/dot_general | solution.py:54
  14.3 0.0 copy-start.1
  14.4 33.5 %all_to_all.10 = bf16[16,32,1792]{2,1,0:T(8,128)(2,1)S(1)} all-to-all(bf16[16,32,1792]{2,1,0:T(8,128)(2,1)S(1)} %bitcast.25), channel_id=1, replica_groups=mesh['dp'=8,'tensor'=16] {'tensor'}, dimensions={0} | all-to-all | bytes 3670016 | tf_op jit(solution)/shard_map/all_to_all | solution.py:62
  47.9 0.0 copy-done.1
  47.9 2.0 %abs_reduce_fusion = (f32[32]{0:T(128)S(1)}, f32[32,1792,16]{1,2,0:T(8,128)S(1)}) fusion(bf16[16,16,1]{0,1,2:T(8,128)(2,1)S(1)} %copy-done.1, bf16[16,32,1792]{2,1,0:T(8,128)(2,1)S(1)} %all_to_all.10), kind=kOutput, calls=%fused_computation.10 | convolution fusion | flops 32112608 | bytes 5505664 | tf_op jit(solution)/shard_map/ea,etf->atf/dot_general | solution.py:59
  49.9 13.3 %fusion.4 = bf16[16,32,1792]{2,0,1:T(8,128)(2,1)S(1)} fusion(f32[32,1792,16]{1,2,0:T(8,128)S(1)} %get-tuple-element.6, f32[32]{0:T(128)S(1)} %broadcast_maximum_fusion), kind=kLoop, calls=%fused_computation.7 | loop fusion | flops 7340032 | bytes 5505152 | tf_op jit(solution)/shard_map/convert_element_type | solution.py:46
  63.2 0.5 copy.9
  63.8 28.0 %all_to_all.11 = bf16[16,32,1792]{2,1,0:T(8,128)(2,1)S(1)} all-to-all(bf16[16,32,1792]{2,1,0:T(8,128)(2,1)S(1)} %copy.9), channel_id=1, replica_groups=mesh['dp'=8,'tensor'=16] {'tensor'}, dimensions={0} | all-to-all | bytes 3670016 | tf_op jit(solution)/shard_map/all_to_all | solution.py:67
  91.8 17.7 %convolution_convert_fusion = bf16[512,6144]{1,0:T(8,128)(2,1)} fusion(bf16[512,1792]{1,0:T(8,128)(2,1)S(1)} %bitcast.26, bf16[1792,6144]{1,0:T(8,128)(2,1)} %param.5), kind=kOutput, calls=%fused_computation | convolution fusion | flops 11277434880 | bytes 30146560 | tf_op jit(solution)/shard_map/dot_general | solution.py:72
  109.5 0.0 reduce-scatter.2.cloned.1.call-update
  109.5 79.3 %reduce-scatter.2.cloned.1.call-done = bf16[32,6144]{1,0:T(8,128)(2,1)} async-done(((bf16[512,6144]{1,0:T(8,128)(2,1)}), bf16[32,6144]{1,0:T(8,128)(2,1)}) %reduce-scatter.2.cloned.1.call-update) | async-done | bytes 393232 | tf_op jit(solution)/shard_map/reduce_scatter | solution.py:71
  (1 shorter events, 0.0 us)
Async XLA Ops:
  6.5 1.5 copy-start
  6.5 182.3 %reduce-scatter.2.cloned.1.call-start = ((), (), s32[]{:S(2)}) async-start(), calls=%async_computation.3 | async-start | bytes 6684672 | tf_op jit(solution)/shard_map/reduce_scatter | solution.py:71
  14.3 33.6 %copy-start.1 = (bf16[16,16,1]{0,1,2:T(8,128)(2,1)S(1)}, bf16[16,16,1]{0,1,2:T(8,128)(2,1)}, u32[]{:S(2)}) copy-start(bf16[16,16,1]{0,1,2:T(8,128)(2,1)} %constant.28) | copy-start | bytes 1540
Sparse Core Ops, SparseCore 0:
  109.6 79.1 reduce-scatter.1
where the time goes:
time: 196 us
  waiting for transfers between devices  79.3 us (40%)
  blocking collectives  61.5 us (31%)
  matrix products  26 us (13%)
  between operations  13.4 us (7%)
  other arithmetic  13.3 us (7%)
  local copies, waits for them, and re-layouts  2.04 us (1%)
    reduce_scatter x1, waiting for transfers between devices, shards(): lax.psum_scatter(jnp.dot(dequant, down_weight, preferred_element_type=jnp...  79.3 us
    all_to_all x1, blocking collectives, shards(): lax.all_to_all(blocks, 'tensor', split_axis=0, concat_axis=0, tiled=True)  33.5 us
    all_to_all x1, blocking collectives, shards(): lax.all_to_all(quantize(rotated, largest), 'tensor', split_axis=0, concat...  28 us
    dot_general x1, matrix products, shards(): jnp.dot(dequant, down_weight, preferred_element_type=jnp.float32)  17.7 us
    convert_element_type x1, other arithmetic, quantize(): return (snapped * token_scale / 7.0).astype(jnp.bfloat16)  13.3 us
    dot_general x1, matrix products, shards(): jnp.dot(activations, rotation, preferred_element_type=jnp.float32)  6.3 us
  transfers between devices with their start and end apart: 1, of which 1 were waited for; matrix products, arithmetic and copies ran while one was open for 0% of the time, Pallas kernels for 0%

commit v1 on v0

v1 whole, which is shorter than its diff:
```python
import functools
import math

import jax
import jax.numpy as jnp
import numpy as np
from jax import lax
from jax.experimental import pallas as pl
from jax.experimental.pallas import tpu as pltpu
from jax.sharding import PartitionSpec as P

MESH = pl.DeviceIdType.MESH
CHUNKS = 2
ROWS = 16
PIECES = 3
WIDE = 1024
TILE = 256
OFFSETS = (
    (0, 1), (1, 0), (0, 3), (3, 0), (1, 1), (3, 3), (1, 3), (3, 1),
    (0, 2), (2, 0), (1, 2), (2, 1), (3, 2), (2, 3), (2, 2),
)


def paley_matrix():
    modulus = 13
    residues = set((value * value % modulus for value in range(1, modulus)))
    confer = np.zeros((14, 14))
    confer[0, 1:] = 1.0
    confer[1:, 0] = 1.0
    for row in range(modulus):
        for col in range(modulus):
            if row != col:
                confer[1 + row, 1 + col] = 1.0 if (col - row) % modulus in residues else -1.0
    return np.kron(confer, np.array([[1.0, 1.0], [1.0, -1.0]])) + np.kron(
        np.eye(14), np.array([[1.0, -1.0], [-1.0, -1.0]])
    )


def sylvester(order):
    matrix = np.ones((1, 1))
    while matrix.shape[0] < order:
        matrix = np.kron(matrix, np.array([[1.0, 1.0], [1.0, -1.0]]))
    return matrix


def sine_coefficients():
    nodes = np.cos(np.pi * (np.arange(64) + 0.5) / 64)
    r2 = 0.125 + 0.125 * nodes
    root = np.sqrt(r2)
    target = np.sinc(2 * root)
    return np.polynomial.chebyshev.Chebyshev.fit(r2, target, 6, domain=[0, 0.25]).convert(
        kind=np.polynomial.Polynomial
    ).coef


SINE = [float(c) for c in sine_coefficients()]


def kernel(
    a_hbm, r_hbm, w_hbm, o_hbm,
    a_in, table, weight, mixed, gathered, rotated, quant, dequant,
    part, far, near, summed, far2, near2, result,
    in_sem, w_sem, send_a, recv_a, send_q, recv_q,
    send1, send2, recv_far, recv_near, recv_far2, recv_near2, out_sem,
):
    me = lax.axis_index("tensor")
    z, y = me // 4, me % 4
    width = a_hbm.shape[-1]
    half = width // 2
    norm = 1.0 / math.sqrt(width * 16)

    def partner(offset):
        return ((z + offset[0]) % 4) * 4 + (y + offset[1]) % 4

    loads = [
        pltpu.make_async_copy(a_hbm.at[:, pl.ds(ROWS * c, ROWS)], a_in.at[c], in_sem.at[c])
        for c in range(CHUNKS)
    ]
    table_load = pltpu.make_async_copy(r_hbm, table, in_sem.at[CHUNKS])
    loads[0].start()
    table_load.start()
    for c in range(1, CHUNKS):
        loads[c].start()
    w_loads = [
        pltpu.make_async_copy(w_hbm.at[:, pl.ds(WIDE * i, WIDE)], weight.at[i], w_sem.at[i])
        for i in range(2 * PIECES)
    ]

    barrier = pltpu.get_barrier_semaphore()
    for offset in OFFSETS:
        pl.semaphore_signal(
            barrier, inc=1, device_id={"tensor": partner(offset)}, device_id_type=MESH
        )

    def rotate(c):
        left = a_in[c, :, :, 0:half].reshape(16 * ROWS, half)
        right = a_in[c, :, :, half:width].reshape(16 * ROWS, half)
        for at in range(0, half, TILE):
            size = min(TILE, half - at)
            cols = table[:, at : at + size]
            first = jnp.dot(left, cols, preferred_element_type=jnp.float32)
            second = jnp.dot(right, cols, preferred_element_type=jnp.float32)
            mixed[c, :, :, at : at + size] = (
                (first + second).astype(jnp.bfloat16).reshape(16, ROWS, size)
            )
            mixed[c, :, :, half + at : half + at + size] = (
                (first - second).astype(jnp.bfloat16).reshape(16, ROWS, size)
            )

    def exchange(c, source, target, send, recv):
        for offset in OFFSETS:
            e = partner(offset)
            pltpu.make_async_remote_copy(
                src_ref=source.at[c, e],
                dst_ref=target.at[c, me],
                send_sem=send.at[c],
                recv_sem=recv.at[c],
                device_id={"tensor": e},
                device_id_type=MESH,
            ).start()
        target[c, me] = source[c, me]

    def exchange_all(c, source, target, send, recv):
        return pltpu.make_async_remote_copy(
            src_ref=source.at[c, pl.ds(0, 15)],
            dst_ref=target.at[c, pl.ds(0, 15)],
            send_sem=send.at[c],
            recv_sem=recv.at[c],
            device_id={"tensor": partner((0, 1))},
            device_id_type=MESH,
        )

    def transform(c):
        def butterfly(t, largest):
            cols = pl.ds(pl.multiple_of(t * 128, 128), 128)
            v = [gathered[c, e, :, cols].astype(jnp.float32) for e in range(16)]
            for bit in (1, 2, 4, 8):
                n = list(v)
                for e in range(16):
                    n[e] = v[e ^ bit] - v[e] if e & bit else v[e] + v[e ^ bit]
                v = n
            for e in range(16):
                rotated[e, :, cols] = v[e]
            m = [jnp.abs(x) for x in v]
            while len(m) > 1:
                m = [jnp.maximum(m[i], m[i + 1]) for i in range(0, len(m), 2)]
            return jnp.maximum(largest, m[0])

        largest = lax.fori_loop(
            0, width // 128, butterfly, jnp.zeros((ROWS, 128), jnp.float32)
        )
        scale = jnp.maximum(jnp.max(largest, axis=1, keepdims=True) * norm, 1.0)
        up = jnp.broadcast_to(7.0 * norm / scale, (ROWS, 128))
        down = jnp.broadcast_to(scale / 7.0, (ROWS, 128))

        def staircase(t, carry):
            cols = pl.ds(pl.multiple_of(t * 128, 128), 128)
            for e in range(16):
                levels = rotated[e, :, cols] * up
                r = levels - jnp.round(levels)
                r2 = r * r
                series = jnp.full_like(r2, SINE[-1])
                for coefficient in SINE[-2::-1]:
                    series = series * r2 + coefficient
                quant[c, e, :, cols] = ((levels - r * series) * down).astype(jnp.bfloat16)
            return carry

        lax.fori_loop(0, width // 128, staircase, 0)

    def axes(h):
        along_y = [partner((0, 1)), partner((0, 3))]
        along_z = [partner((1, 0)), partner((3, 0))]
        return (y, z, along_y, along_z) if h == 0 else (z, y, along_z, along_y)

    def send(source, target, s, r, e):
        pltpu.make_async_remote_copy(
            src_ref=source, dst_ref=target, send_sem=s, recv_sem=r,
            device_id={"tensor": e}, device_id_type=MESH,
        ).start()

    order = [(c, p, h) for c in range(CHUNKS) for p in range(PIECES) for h in range(2)]

    def project(g):
        c, p, h = order[g]
        i = h * PIECES + p
        if c == 0:
            w_loads[i].wait()

        def tile(n, carry):
            cols = pl.ds(pl.multiple_of(n * TILE, TILE), TILE)
            product = jnp.dot(
                dequant[c].reshape(16 * ROWS, width),
                weight[i, :, cols],
                preferred_element_type=jnp.float32,
            ).astype(jnp.bfloat16)
            for e in range(16):
                u, v = (e % 4, e // 4) if h == 0 else (e // 4, e % 4)
                part[g, u, v, :, cols] = product[e * ROWS : (e + 1) * ROWS]
            return carry

        lax.fori_loop(0, WIDE // TILE, tile, 0)
        u, v, first, second = axes(h)
        up, down, opposite = (u + 1) % 4, (u + 3) % 4, (u + 2) % 4
        low, high = pl.ds(0, 2), pl.ds(2, 2)
        send(part.at[g, opposite, low], far.at[g, 0], send1.at[g], recv_far.at[g], first[0])
        send(part.at[g, opposite, high], far.at[g, 1], send1.at[g], recv_far.at[g], first[1])
        send(part.at[g, up, high], near.at[g, 0, high], send1.at[g], recv_near.at[g], first[0])
        send(part.at[g, down, low], near.at[g, 1, low], send1.at[g], recv_near.at[g], first[1])

    def fake(source, target, s, r):
        return pltpu.make_async_remote_copy(
            src_ref=source, dst_ref=target, send_sem=s, recv_sem=r,
            device_id={"tensor": partner((0, 1))}, device_id_type=MESH,
        )

    def relay(g):
        c, p, h = order[g]
        u, v, first, second = axes(h)
        up, down = (u + 1) % 4, (u + 3) % 4
        fake(far.at[g], far.at[g], send1.at[g], recv_far.at[g]).wait_recv()
        for k in range(2):
            part[g, up, k] = (
                part[g, up, k].astype(jnp.float32) + far[g, 0, k].astype(jnp.float32)
            ).astype(jnp.bfloat16)
            part[g, down, 2 + k] = (
                part[g, down, 2 + k].astype(jnp.float32) + far[g, 1, k].astype(jnp.float32)
            ).astype(jnp.bfloat16)
        low, high = pl.ds(0, 2), pl.ds(2, 2)
        send(part.at[g, up, low], near.at[g, 0, low], send1.at[g], recv_near.at[g], first[0])
        send(part.at[g, down, high], near.at[g, 1, high], send1.at[g], recv_near.at[g], first[1])

    def gather(g):
        c, p, h = order[g]
        u, v, first, second = axes(h)
        fake(near.at[g], near.at[g], send1.at[g], recv_near.at[g]).wait_recv()
        for k in range(4):
            summed[g, k] = (
                part[g, u, k].astype(jnp.float32)
                + near[g, 0, k].astype(jnp.float32)
                + near[g, 1, k].astype(jnp.float32)
            ).astype(jnp.bfloat16)
        up, down, opposite = (v + 1) % 4, (v + 3) % 4, (v + 2) % 4
        low, high = pl.ds(0, WIDE // 2), pl.ds(WIDE // 2, WIDE // 2)
        send(summed.at[g, opposite, :, low], far2.at[g, 0], send2.at[g], recv_far2.at[g], second[0])
        send(summed.at[g, opposite, :, high], far2.at[g, 1], send2.at[g], recv_far2.at[g], second[1])
        send(summed.at[g, up, :, high], near2.at[g, 0, :, high], send2.at[g], recv_near2.at[g], second[0])
        send(summed.at[g, down, :, low], near2.at[g, 1, :, low], send2.at[g], recv_near2.at[g], second[1])

    def relay2(g):
        c, p, h = order[g]
        u, v, first, second = axes(h)
        up, down = (v + 1) % 4, (v + 3) % 4
        low, high = pl.ds(0, WIDE // 2), pl.ds(WIDE // 2, WIDE // 2)
        fake(far2.at[g], far2.at[g], send2.at[g], recv_far2.at[g]).wait_recv()
        summed[g, up, :, low] = (
            summed[g, up, :, low].astype(jnp.float32) + far2[g, 0].astype(jnp.float32)
        ).astype(jnp.bfloat16)
        summed[g, down, :, high] = (
            summed[g, down, :, high].astype(jnp.float32) + far2[g, 1].astype(jnp.float32)
        ).astype(jnp.bfloat16)
        send(summed.at[g, up, :, low], near2.at[g, 0, :, low], send2.at[g], recv_near2.at[g], second[0])
        send(summed.at[g, down, :, high], near2.at[g, 1, :, high], send2.at[g], recv_near2.at[g], second[1])

    def out_copy(g):
        c, p, h = order[g]
        at = (h * PIECES + p) * WIDE
        return pltpu.make_async_copy(
            result.at[g],
            o_hbm.at[pl.ds(c * ROWS, ROWS), pl.ds(at, WIDE)],
            out_sem.at[g],
        )

    def finish(g):
        c, p, h = order[g]
        u, v, first, second = axes(h)
        fake(near2.at[g], near2.at[g], send2.at[g], recv_near2.at[g]).wait_recv()
        result[g] = (
            summed[g, v].astype(jnp.float32)
            + near2[g, 0].astype(jnp.float32)
            + near2[g, 1].astype(jnp.float32)
        ).astype(jnp.bfloat16)
        out_copy(g).start()

    table_load.wait()
    loads[0].wait()
    rotate(0)
    pl.semaphore_wait(barrier, len(OFFSETS))
    exchange(0, mixed, gathered, send_a, recv_a)
    loads[1].wait()
    rotate(1)
    exchange(1, mixed, gathered, send_a, recv_a)
    for load in w_loads:
        load.start()
    for c in range(CHUNKS):
        exchange_all(c, mixed, gathered, send_a, recv_a).wait_recv()
        transform(c)
        exchange(c, quant, dequant, send_q, recv_q)
    each = PIECES * 2
    exchange_all(0, quant, dequant, send_q, recv_q).wait_recv()
    for g in range(each):
        project(g)
    exchange_all(1, quant, dequant, send_q, recv_q).wait_recv()
    for g in range(each):
        project(each + g)
        relay(g)
    for g in range(each):
        relay(each + g)
        gather(g)
    for g in range(each):
        relay2(g)
        gather(each + g)
        finish(g)
    for g in range(each):
        relay2(each + g)
    for g in range(each):
        finish(each + g)

    for c in range(CHUNKS):
        exchange_all(c, mixed, gathered, send_a, recv_a).wait_send()
        exchange_all(c, quant, dequant, send_q, recv_q).wait_send()
    for g in range(2 * each):
        fake(part.at[g, pl.ds(0, 3)], part.at[g, pl.ds(0, 3)], send1.at[g], recv_far.at[g]).wait_send()
        fake(summed.at[g, pl.ds(0, 3)], summed.at[g, pl.ds(0, 3)], send2.at[g], recv_far2.at[g]).wait_send()
        out_copy(g).wait()


def shards(activations, down_weight):
    count_rows, width = activations.shape
    features = down_weight.shape[1]
    table = jnp.asarray(np.kron(sylvester(32), paley_matrix()), jnp.bfloat16)
    bf16, f32 = jnp.bfloat16, jnp.float32
    groups = CHUNKS * PIECES * 2
    dma = pltpu.SemaphoreType.DMA
    any_space = pl.BlockSpec(memory_space=pl.ANY)
    return pl.pallas_call(
        kernel,
        out_shape=jax.ShapeDtypeStruct((count_rows // 16, features), bf16),
        in_specs=[any_space] * 3,
        out_specs=any_space,
        scratch_shapes=[
            pltpu.VMEM((CHUNKS, 16, ROWS, width), bf16),
            pltpu.VMEM(table.shape, bf16),
            pltpu.VMEM((2 * PIECES, width, WIDE), bf16),
            pltpu.VMEM((CHUNKS, 16, ROWS, width), bf16),
            pltpu.VMEM((CHUNKS, 16, ROWS, width), bf16),
            pltpu.VMEM((16, ROWS, width), f32),
            pltpu.VMEM((CHUNKS, 16, ROWS, width), bf16),
            pltpu.VMEM((CHUNKS, 16, ROWS, width), bf16),
            pltpu.VMEM((groups, 4, 4, ROWS, WIDE), bf16),
            pltpu.VMEM((groups, 2, 2, ROWS, WIDE), bf16),
            pltpu.VMEM((groups, 2, 4, ROWS, WIDE), bf16),
            pltpu.VMEM((groups, 4, ROWS, WIDE), bf16),
            pltpu.VMEM((groups, 2, ROWS, WIDE // 2), bf16),
            pltpu.VMEM((groups, 2, ROWS, WIDE), bf16),
            pltpu.VMEM((groups, ROWS, WIDE), bf16),
            dma((CHUNKS + 1,)),
            dma((2 * PIECES,)),
            dma((CHUNKS,)), dma((CHUNKS,)), dma((CHUNKS,)), dma((CHUNKS,)),
            dma((groups,)), dma((groups,)),
            dma((groups,)), dma((groups,)), dma((groups,)), dma((groups,)),
            dma((groups,)),
        ],
        compiler_params=pltpu.CompilerParams(
            collective_id=0, has_side_effects=True, vmem_limit_bytes=62 * 2**20
        ),
        name="rotate_quantize_project",
    )(activations.reshape(16, count_rows // 16, width), table, down_weight)


def solution(mesh):
    placed = (P("dp", "tensor"), P("tensor", None))
    return jax.shard_map(
        shards, mesh=mesh, in_specs=placed, out_specs=P(("dp", "tensor"), None), check_vma=False
    )
```

time: 196 us -> 101 us (0.52)
  Pallas kernels: 0 us -> 98.8 us
  waiting for transfers between devices: 79.3 us -> 0 us
  blocking collectives: 61.5 us -> 0 us
  matrix products: 26 us -> 0 us
  between operations: 13.4 us -> 0.01 us
  other arithmetic: 13.3 us -> 0 us
    pallas_call x0 -> x1, Pallas kernels: none -> 98.8 us  [shards(): pl.pallas_call(kernel, out_shape=jax.ShapeDtypeStruct((count_rows // 16,...]
    reduce_scatter x1 -> x0, waiting for transfers between devices: 79.3 us -> none  [shards(): lax.psum_scatter(jnp.dot(dequant, down_weight, preferred_element_type=jnp...]
    all_to_all x2 -> x0, blocking collectives: 61.5 us -> none  [the longest x1 33.5 us: shards(): lax.all_to_all(blocks, 'tensor', split_axis=0, concat_axis=0, tiled=True)]
    dot_general x3 -> x0, matrix products: 26 us -> none  [the longest x1 17.7 us: shards(): jnp.dot(dequant, down_weight, preferred_element_type=jnp.float32)]
    convert_element_type x1 -> x0, other arithmetic: 13.3 us -> none  [quantize(): return (snapped * token_scale / 7.0).astype(jnp.bfloat16)]
  transfers between devices with their start and end apart: 1 -> 0, of which waited for: 1 -> 0; matrix products, arithmetic and copies ran while one was open for 0% -> 0% of each run, Pallas kernels for 0% -> 0%
where the time goes in v1:
time: 101 us
  Pallas kernels  98.8 us (98%)
  local copies, waits for them, and re-layouts  1.77 us (2%)
    pallas_call x1, Pallas kernels, shards(): pl.pallas_call(kernel, out_shape=jax.ShapeDtypeStruct((count_rows // 16,...  98.8 us

profile of v1, /device:TPU:0, one launch (start us, length us, event | category | flops | bytes accessed | tf_op | source)
XLA Modules:
  0.0 100.6 jit_solution(9377560309610832356)
XLA Ops:
  0.0 98.8 %rotate_quantize_project.1 = bf16[32,6144]{1,0:T(8,128)(2,1)} custom-call(bf16[16,32,1792]{2,1,0:T(8,128)(2,1)} %bitcast.1, bf16[896,896]{1,0:T(8,128)(2,1)} %constant.2.clone.r_hbm, bf16[1792,6144]{1,0:T(8,128)(2,1)} %w_hbm.1), custom_call_target="tpu_custom_call" | custom-call | tf_op jit(solution)/shard_map/rotate_quantize_project/pallas_call | solution.py:335
  98.8 1.8 %copy.5 = bf16[32,6144]{1,0:T(8,128)(2,1)} copy(bf16[32,6144]{1,0:T(8,128)(2,1)} %rotate_quantize_project.1) | data formatting | bytes 786432

commit v2 on v1

--- a/solution.py
+++ b/solution.py
@@ -180,7 +180,28 @@
 
     order = [(c, p, h) for c in range(CHUNKS) for p in range(PIECES) for h in range(2)]
 
-    def project(g):
+    def project(k):
+        for g in (2 * k, 2 * k + 1):
+            multiply(g)
+        flows = [[], []]
+        for h in range(2):
+            g = 2 * k + h
+            u, v, first, second = axes(h)
+            up, down, opposite = (u + 1) % 4, (u + 3) % 4, (u + 2) % 4
+            flows[h] = [
+                (part.at[g, opposite, low], far.at[g, 0], send1.at[g], recv_far.at[g], first[0]),
+                (part.at[g, opposite, high], far.at[g, 1], send1.at[g], recv_far.at[g], first[1]),
+                (part.at[g, up, high], near.at[g, 0, high], send1.at[g], recv_near.at[g], first[0]),
+                (part.at[g, down, low], near.at[g, 1, low], send1.at[g], recv_near.at[g], first[1]),
+            ]
+        interleave(flows)
+
+    def interleave(flows):
+        for pair in zip(*flows):
+            for flow in pair:
+                send(*flow)
+
+    def multiply(g):
         c, p, h = order[g]
         i = h * PIECES + p
         if c == 0:
@@ -199,13 +220,6 @@
             return carry
 
         lax.fori_loop(0, WIDE // TILE, tile, 0)
-        u, v, first, second = axes(h)
-        up, down, opposite = (u + 1) % 4, (u + 3) % 4, (u + 2) % 4
-        low, high = pl.ds(0, 2), pl.ds(2, 2)
-        send(part.at[g, opposite, low], far.at[g, 0], send1.at[g], recv_far.at[g], first[0])
-        send(part.at[g, opposite, high], far.at[g, 1], send1.at[g], recv_far.at[g], first[1])
-        send(part.at[g, up, high], near.at[g, 0, high], send1.at[g], recv_near.at[g], first[0])
-        send(part.at[g, down, low], near.at[g, 1, low], send1.at[g], recv_near.at[g], first[1])
 
     def fake(source, target, s, r):
         return pltpu.make_async_remote_copy(
@@ -213,53 +227,68 @@
             device_id={"tensor": partner((0, 1))}, device_id_type=MESH,
         )
 
-    def relay(g):
-        c, p, h = order[g]
-        u, v, first, second = axes(h)
-        up, down = (u + 1) % 4, (u + 3) % 4
-        fake(far.at[g], far.at[g], send1.at[g], recv_far.at[g]).wait_recv()
-        for k in range(2):
-            part[g, up, k] = (
-                part[g, up, k].astype(jnp.float32) + far[g, 0, k].astype(jnp.float32)
+    low, high = pl.ds(0, 2), pl.ds(2, 2)
+    left, right = pl.ds(0, WIDE // 2), pl.ds(WIDE // 2, WIDE // 2)
+
+    def relay(k):
+        flows = [[], []]
+        for h in range(2):
+            g = 2 * k + h
+            u, v, first, second = axes(h)
+            up, down = (u + 1) % 4, (u + 3) % 4
+            fake(far.at[g], far.at[g], send1.at[g], recv_far.at[g]).wait_recv()
+            for j in range(2):
+                part[g, up, j] = (
+                    part[g, up, j].astype(jnp.float32) + far[g, 0, j].astype(jnp.float32)
+                ).astype(jnp.bfloat16)
+                part[g, down, 2 + j] = (
+                    part[g, down, 2 + j].astype(jnp.float32) + far[g, 1, j].astype(jnp.float32)
+                ).astype(jnp.bfloat16)
+            flows[h] = [
+                (part.at[g, up, low], near.at[g, 0, low], send1.at[g], recv_near.at[g], first[0]),
+                (part.at[g, down, high], near.at[g, 1, high], send1.at[g], recv_near.at[g], first[1]),
+            ]
+        interleave(flows)
+
+    def gather(k):
+        flows = [[], []]
+        for h in range(2):
+            g = 2 * k + h
+            u, v, first, second = axes(h)
+            fake(near.at[g], near.at[g], send1.at[g], recv_near.at[g]).wait_recv()
+            for j in range(4):
+                summed[g, j] = (
+                    part[g, u, j].astype(jnp.float32)
+                    + near[g, 0, j].astype(jnp.float32)
+                    + near[g, 1, j].astype(jnp.float32)
+                ).astype(jnp.bfloat16)
+            up, down, opposite = (v + 1) % 4, (v + 3) % 4, (v + 2) % 4
+            flows[h] = [
+                (summed.at[g, opposite, :, left], far2.at[g, 0], send2.at[g], recv_far2.at[g], second[0]),
+                (summed.at[g, opposite, :, right], far2.at[g, 1], send2.at[g], recv_far2.at[g], second[1]),
+                (summed.at[g, up, :, right], near2.at[g, 0, :, right], send2.at[g], recv_near2.at[g], second[0]),
+                (summed.at[g, down, :, left], near2.at[g, 1, :, left], send2.at[g], recv_near2.at[g], second[1]),
+            ]
+        interleave(flows)
+
+    def relay2(k):
+        flows = [[], []]
+        for h in range(2):
+            g = 2 * k + h
+            u, v, first, second = axes(h)
+            up, down = (v + 1) % 4, (v + 3) % 4
+            fake(far2.at[g], far2.at[g], send2.at[g], recv_far2.at[g]).wait_recv()
+            summed[g, up, :, left] = (
+                summed[g, up, :, left].astype(jnp.float32) + far2[g, 0].astype(jnp.float32)
             ).astype(jnp.bfloat16)
-            part[g, down, 2 + k] = (
-                part[g, down, 2 + k].astype(jnp.float32) + far[g, 1, k].astype(jnp.float32)
+            summed[g, down, :, right] = (
+                summed[g, down, :, right].astype(jnp.float32) + far2[g, 1].astype(jnp.float32)
             ).astype(jnp.bfloat16)
-        low, high = pl.ds(0, 2), pl.ds(2, 2)
-        send(part.at[g, up, low], near.at[g, 0, low], send1.at[g], recv_near.at[g], first[0])
-        send(part.at[g, down, high], near.at[g, 1, high], send1.at[g], recv_near.at[g], first[1])
-
-    def gather(g):
-        c, p, h = order[g]
-        u, v, first, second = axes(h)
-        fake(near.at[g], near.at[g], send1.at[g], recv_near.at[g]).wait_recv()
-        for k in range(4):
-            summed[g, k] = (
-                part[g, u, k].astype(jnp.float32)
-                + near[g, 0, k].astype(jnp.float32)
-                + near[g, 1, k].astype(jnp.float32)
-            ).astype(jnp.bfloat16)
-        up, down, opposite = (v + 1) % 4, (v + 3) % 4, (v + 2) % 4
-        low, high = pl.ds(0, WIDE // 2), pl.ds(WIDE // 2, WIDE // 2)
-        send(summed.at[g, opposite, :, low], far2.at[g, 0], send2.at[g], recv_far2.at[g], second[0])
-        send(summed.at[g, opposite, :, high], far2.at[g, 1], send2.at[g], recv_far2.at[g], second[1])
-        send(summed.at[g, up, :, high], near2.at[g, 0, :, high], send2.at[g], recv_near2.at[g], second[0])
-        send(summed.at[g, down, :, low], near2.at[g, 1, :, low], send2.at[g], recv_near2.at[g], second[1])
-
-    def relay2(g):
-        c, p, h = order[g]
-        u, v, first, second = axes(h)
-        up, down = (v + 1) % 4, (v + 3) % 4
-        low, high = pl.ds(0, WIDE // 2), pl.ds(WIDE // 2, WIDE // 2)
-        fake(far2.at[g], far2.at[g], send2.at[g], recv_far2.at[g]).wait_recv()
-        summed[g, up, :, low] = (
-            summed[g, up, :, low].astype(jnp.float32) + far2[g, 0].astype(jnp.float32)
-        ).astype(jnp.bfloat16)
-        summed[g, down, :, high] = (
-            summed[g, down, :, high].astype(jnp.float32) + far2[g, 1].astype(jnp.float32)
-        ).astype(jnp.bfloat16)
-        send(summed.at[g, up, :, low], near2.at[g, 0, :, low], send2.at[g], recv_near2.at[g], second[0])
-        send(summed.at[g, down, :, high], near2.at[g, 1, :, high], send2.at[g], recv_near2.at[g], second[1])
+            flows[h] = [
+                (summed.at[g, up, :, left], near2.at[g, 0, :, left], send2.at[g], recv_near2.at[g], second[0]),
+                (summed.at[g, down, :, right], near2.at[g, 1, :, right], send2.at[g], recv_near2.at[g], second[1]),
+            ]
+        interleave(flows)
 
     def out_copy(g):
         c, p, h = order[g]
@@ -270,16 +299,17 @@
             out_sem.at[g],
         )
 
-    def finish(g):
-        c, p, h = order[g]
-        u, v, first, second = axes(h)
-        fake(near2.at[g], near2.at[g], send2.at[g], recv_near2.at[g]).wait_recv()
-        result[g] = (
-            summed[g, v].astype(jnp.float32)
-            + near2[g, 0].astype(jnp.float32)
-            + near2[g, 1].astype(jnp.float32)
-        ).astype(jnp.bfloat16)
-        out_copy(g).start()
+    def finish(k):
+        for h in range(2):
+            g = 2 * k + h
+            u, v, first, second = axes(h)
+            fake(near2.at[g], near2.at[g], send2.at[g], recv_near2.at[g]).wait_recv()
+            result[g] = (
+                summed[g, v].astype(jnp.float32)
+                + near2[g, 0].astype(jnp.float32)
+                + near2[g, 1].astype(jnp.float32)
+            ).astype(jnp.bfloat16)
+            out_copy(g).start()
 
     table_load.wait()
     loads[0].wait()
@@ -295,7 +325,7 @@
         exchange_all(c, mixed, gathered, send_a, recv_a).wait_recv()
         transform(c)
         exchange(c, quant, dequant, send_q, recv_q)
-    each = PIECES * 2
+    each = PIECES
     exchange_all(0, quant, dequant, send_q, recv_q).wait_recv()
     for g in range(each):
         project(g)
@@ -318,7 +348,7 @@
     for c in range(CHUNKS):
         exchange_all(c, mixed, gathered, send_a, recv_a).wait_send()
         exchange_all(c, quant, dequant, send_q, recv_q).wait_send()
-    for g in range(2 * each):
+    for g in range(len(order)):
         fake(part.at[g, pl.ds(0, 3)], part.at[g, pl.ds(0, 3)], send1.at[g], recv_far.at[g]).wait_send()
         fake(summed.at[g, pl.ds(0, 3)], summed.at[g, pl.ds(0, 3)], send2.at[g], recv_far2.at[g]).wait_send()
         out_copy(g).wait()

time: 101 us -> 91.3 us (0.904)
  Pallas kernels: 98.8 us -> 89.4 us
    pallas_call x1, Pallas kernels: 98.8 us -> 89.4 us  [shards(): pl.pallas_call(kernel, out_shape=jax.ShapeDtypeStruct((count_rows // 16,...]
where the time goes in v2:
time: 91.3 us; the launch traced here: 91.2 us
  Pallas kernels  89.4 us (98%)
  local copies, waits for them, and re-layouts  1.77 us (2%)
    pallas_call x1, Pallas kernels, shards(): pl.pallas_call(kernel, out_shape=jax.ShapeDtypeStruct((count_rows // 16,...  89.4 us

profile of v2, /device:TPU:0, one launch (start us, length us, event | category | flops | bytes accessed | tf_op | source)
XLA Modules:
  0.0 91.2 jit_solution(4410946122946743573)
XLA Ops:
  0.0 89.4 %rotate_quantize_project.1 = bf16[32,6144]{1,0:T(8,128)(2,1)} custom-call(bf16[16,32,1792]{2,1,0:T(8,128)(2,1)} %bitcast.1, bf16[896,896]{1,0:T(8,128)(2,1)} %constant.2.clone.r_hbm, bf16[1792,6144]{1,0:T(8,128)(2,1)} %w_hbm.1), custom_call_target="tpu_custom_call" | custom-call | tf_op jit(solution)/shard_map/rotate_quantize_project/pallas_call | solution.py:365
  89.4 1.8 %copy.5 = bf16[32,6144]{1,0:T(8,128)(2,1)} copy(bf16[32,6144]{1,0:T(8,128)(2,1)} %rotate_quantize_project.1) | data formatting | bytes 786432

commit v3 on v2

--- a/solution.py
+++ b/solution.py
@@ -14,10 +14,12 @@
 ROWS = 16
 PIECES = 3
 WIDE = 1024
-TILE = 256
+DIRECT = (3, 4, 5)
 OFFSETS = (
-    (0, 1), (1, 0), (0, 3), (3, 0), (1, 1), (3, 3), (1, 3), (3, 1),
-    (0, 2), (2, 0), (1, 2), (2, 1), (3, 2), (2, 3), (2, 2),
+    ((0, 1), (1, 0), (0, 3), (3, 0)),
+    ((1, 1), (3, 3), (1, 3), (3, 1), (0, 2), (2, 0)),
+    ((1, 2), (2, 1), (3, 2), (2, 3)),
+    ((2, 2),),
 )
 
 
@@ -61,7 +63,7 @@
     a_in, table, weight, mixed, gathered, rotated, quant, dequant,
     part, far, near, summed, far2, near2, result,
     in_sem, w_sem, send_a, recv_a, send_q, recv_q,
-    send1, send2, recv_far, recv_near, recv_far2, recv_near2, out_sem,
+    send1, send2, recv_far, recv_near, recv_far2, recv_near2, out_sem, heard,
 ):
     me = lax.axis_index("tensor")
     z, y = me // 4, me % 4
@@ -87,16 +89,25 @@
     ]
 
     barrier = pltpu.get_barrier_semaphore()
-    for offset in OFFSETS:
+    for offset in OFFSETS[0]:
         pl.semaphore_signal(
             barrier, inc=1, device_id={"tensor": partner(offset)}, device_id_type=MESH
         )
 
+    def hear(stage):
+        pl.semaphore_wait(barrier if stage == 0 else heard.at[stage - 1], 4)
+        if stage < 3:
+            for offset in OFFSETS[0]:
+                pl.semaphore_signal(
+                    heard.at[stage], inc=1,
+                    device_id={"tensor": partner(offset)}, device_id_type=MESH,
+                )
+
     def rotate(c):
         left = a_in[c, :, :, 0:half].reshape(16 * ROWS, half)
         right = a_in[c, :, :, half:width].reshape(16 * ROWS, half)
-        for at in range(0, half, TILE):
-            size = min(TILE, half - at)
+        for at in range(0, half, 256):
+            size = min(256, half - at)
             cols = table[:, at : at + size]
             first = jnp.dot(left, cols, preferred_element_type=jnp.float32)
             second = jnp.dot(right, cols, preferred_element_type=jnp.float32)
@@ -107,8 +118,8 @@
                 (first - second).astype(jnp.bfloat16).reshape(16, ROWS, size)
             )
 
-    def exchange(c, source, target, send, recv):
-        for offset in OFFSETS:
+    def exchange(c, stages, source, target, send, recv):
+        for offset in sum((OFFSETS[stage] for stage in stages), ()):
             e = partner(offset)
             pltpu.make_async_remote_copy(
                 src_ref=source.at[c, e],
@@ -118,7 +129,6 @@
                 device_id={"tensor": e},
                 device_id_type=MESH,
             ).start()
-        target[c, me] = source[c, me]
 
     def exchange_all(c, source, target, send, recv):
         return pltpu.make_async_remote_copy(
@@ -168,8 +178,8 @@
         lax.fori_loop(0, width // 128, staircase, 0)
 
     def axes(h):
-        along_y = [partner((0, 1)), partner((0, 3))]
-        along_z = [partner((1, 0)), partner((3, 0))]
+        along_y = [partner((0, 1)), partner((0, 3)), partner((0, 2))]
+        along_z = [partner((1, 0)), partner((3, 0)), partner((2, 0))]
         return (y, z, along_y, along_z) if h == 0 else (z, y, along_z, along_y)
 
     def send(source, target, s, r, e):
@@ -207,19 +217,12 @@
         if c == 0:
             w_loads[i].wait()
 
-        def tile(n, carry):
-            cols = pl.ds(pl.multiple_of(n * TILE, TILE), TILE)
-            product = jnp.dot(
-                dequant[c].reshape(16 * ROWS, width),
-                weight[i, :, cols],
-                preferred_element_type=jnp.float32,
-            ).astype(jnp.bfloat16)
-            for e in range(16):
-                u, v = (e % 4, e // 4) if h == 0 else (e // 4, e % 4)
-                part[g, u, v, :, cols] = product[e * ROWS : (e + 1) * ROWS]
-            return carry
-
-        lax.fori_loop(0, WIDE // TILE, tile, 0)
+        product = jnp.dot(
+            dequant[c].reshape(16 * ROWS, width), weight[i], preferred_element_type=jnp.float32
+        ).astype(jnp.bfloat16)
+        for e in range(16):
+            u, v = (e % 4, e // 4) if h == 0 else (e // 4, e % 4)
+            part[g, u, v] = product[e * ROWS : (e + 1) * ROWS]
 
     def fake(source, target, s, r):
         return pltpu.make_async_remote_copy(
@@ -263,6 +266,13 @@
                     + near[g, 1, j].astype(jnp.float32)
                 ).astype(jnp.bfloat16)
             up, down, opposite = (v + 1) % 4, (v + 3) % 4, (v + 2) % 4
+            if k in DIRECT:
+                flows[h] = [
+                    (summed.at[g, opposite], near2.at[g, 2], send2.at[g], recv_near2.at[g], second[2]),
+                    (summed.at[g, up], near2.at[g, 0], send2.at[g], recv_near2.at[g], second[0]),
+                    (summed.at[g, down], near2.at[g, 1], send2.at[g], recv_near2.at[g], second[1]),
+                ]
+                continue
             flows[h] = [
                 (summed.at[g, opposite, :, left], far2.at[g, 0], send2.at[g], recv_far2.at[g], second[0]),
                 (summed.at[g, opposite, :, right], far2.at[g, 1], send2.at[g], recv_far2.at[g], second[1]),
@@ -272,6 +282,8 @@
         interleave(flows)
 
     def relay2(k):
+        if k in DIRECT:
+            return
         flows = [[], []]
         for h in range(2):
             g = 2 * k + h
@@ -303,28 +315,35 @@
         for h in range(2):
             g = 2 * k + h
             u, v, first, second = axes(h)
-            fake(near2.at[g], near2.at[g], send2.at[g], recv_near2.at[g]).wait_recv()
-            result[g] = (
-                summed[g, v].astype(jnp.float32)
-                + near2[g, 0].astype(jnp.float32)
-                + near2[g, 1].astype(jnp.float32)
-            ).astype(jnp.bfloat16)
+            count = 3 if k in DIRECT else 2
+            landed = near2.at[g, pl.ds(0, count)]
+            fake(landed, landed, send2.at[g], recv_near2.at[g]).wait_recv()
+            total = summed[g, v].astype(jnp.float32)
+            for j in range(count):
+                total = total + near2[g, j].astype(jnp.float32)
+            result[g] = total.astype(jnp.bfloat16)
             out_copy(g).start()
 
+    hear(0)
     table_load.wait()
     loads[0].wait()
     rotate(0)
-    pl.semaphore_wait(barrier, len(OFFSETS))
-    exchange(0, mixed, gathered, send_a, recv_a)
-    loads[1].wait()
-    rotate(1)
-    exchange(1, mixed, gathered, send_a, recv_a)
+    for stage in range(4):
+        if stage > 0:
+            hear(stage)
+        exchange(0, (stage,), mixed, gathered, send_a, recv_a)
+        if stage == 1:
+            loads[1].wait()
+            rotate(1)
+    exchange(1, range(4), mixed, gathered, send_a, recv_a)
     for load in w_loads:
         load.start()
     for c in range(CHUNKS):
+        gathered[c, me] = mixed[c, me]
         exchange_all(c, mixed, gathered, send_a, recv_a).wait_recv()
         transform(c)
-        exchange(c, quant, dequant, send_q, recv_q)
+        exchange(c, range(4), quant, dequant, send_q, recv_q)
+        dequant[c, me] = quant[c, me]
     each = PIECES
     exchange_all(0, quant, dequant, send_q, recv_q).wait_recv()
     for g in range(each):
@@ -339,8 +358,8 @@
     for g in range(each):
         relay2(g)
         gather(each + g)
+    for g in range(each):
         finish(g)
-    for g in range(each):
         relay2(each + g)
     for g in range(each):
         finish(each + g)
@@ -381,7 +400,7 @@
             pltpu.VMEM((groups, 2, 4, ROWS, WIDE), bf16),
             pltpu.VMEM((groups, 4, ROWS, WIDE), bf16),
             pltpu.VMEM((groups, 2, ROWS, WIDE // 2), bf16),
-            pltpu.VMEM((groups, 2, ROWS, WIDE), bf16),
+            pltpu.VMEM((groups, 3, ROWS, WIDE), bf16),
             pltpu.VMEM((groups, ROWS, WIDE), bf16),
             dma((CHUNKS + 1,)),
             dma((2 * PIECES,)),
@@ -389,6 +408,7 @@
             dma((groups,)), dma((groups,)),
             dma((groups,)), dma((groups,)), dma((groups,)), dma((groups,)),
             dma((groups,)),
+            pltpu.SemaphoreType.REGULAR((3,)),
         ],
         compiler_params=pltpu.CompilerParams(
             collective_id=0, has_side_effects=True, vmem_limit_bytes=62 * 2**20

time: 91.3 us -> 84.5 us (0.926)
  Pallas kernels: 89.4 us -> 82.6 us
    pallas_call x1, Pallas kernels: 89.4 us -> 82.6 us  [shards(): pl.pallas_call(kernel, out_shape=jax.ShapeDtypeStruct((count_rows // 16,...]
where the time goes in v3:
time: 84.5 us; the launch traced here: 84.4 us
  Pallas kernels  82.6 us (98%)
  local copies, waits for them, and re-layouts  1.77 us (2%)
    pallas_call x1, Pallas kernels, shards(): pl.pallas_call(kernel, out_shape=jax.ShapeDtypeStruct((count_rows // 16,...  82.6 us
    unnamed x1, local copies, waits for them, and re-layouts  1.77 us

profile of v3, /device:TPU:0, one launch (start us, length us, event | category | flops | bytes accessed | tf_op | source)
XLA Modules:
  0.0 84.4 jit_solution(4394499284413685378)
XLA Ops:
  0.0 82.6 %rotate_quantize_project.1 = bf16[32,6144]{1,0:T(8,128)(2,1)} custom-call(bf16[16,32,1792]{2,1,0:T(8,128)(2,1)} %bitcast.1, bf16[896,896]{1,0:T(8,128)(2,1)} %constant.2.clone.r_hbm, bf16[1792,6144]{1,0:T(8,128)(2,1)} %w_hbm.1), custom_call_target="tpu_custom_call" | custom-call | tf_op jit(solution)/shard_map/rotate_quantize_project/pallas_call | solution.py:384
  82.6 1.8 %copy.5 = bf16[32,6144]{1,0:T(8,128)(2,1)} copy(bf16[32,6144]{1,0:T(8,128)(2,1)} %rotate_quantize_project.1) | data formatting | bytes 786432

commit v4 on v3

--- a/solution.py
+++ b/solution.py
@@ -59,11 +59,11 @@
 
 
 def kernel(
-    a_hbm, r_hbm, w_hbm, o_hbm,
+    a_hbm, r_hbm, w_hbm, out,
     a_in, table, weight, mixed, gathered, rotated, quant, dequant,
-    part, far, near, summed, far2, near2, result,
+    part, far, near, summed, far2, near2,
     in_sem, w_sem, send_a, recv_a, send_q, recv_q,
-    send1, send2, recv_far, recv_near, recv_far2, recv_near2, out_sem, heard,
+    send1, send2, recv_far, recv_near, recv_far2, recv_near2, heard,
 ):
     me = lax.axis_index("tensor")
     z, y = me // 4, me % 4
@@ -103,20 +103,20 @@
                     device_id={"tensor": partner(offset)}, device_id_type=MESH,
                 )
 
-    def rotate(c):
-        left = a_in[c, :, :, 0:half].reshape(16 * ROWS, half)
-        right = a_in[c, :, :, half:width].reshape(16 * ROWS, half)
+    def rotate(c, places):
+        rows = [a_in[c, e] for e in places]
+        left = jnp.concatenate([row[:, 0:half] for row in rows], axis=0)
+        right = jnp.concatenate([row[:, half:width] for row in rows], axis=0)
         for at in range(0, half, 256):
             size = min(256, half - at)
             cols = table[:, at : at + size]
             first = jnp.dot(left, cols, preferred_element_type=jnp.float32)
             second = jnp.dot(right, cols, preferred_element_type=jnp.float32)
-            mixed[c, :, :, at : at + size] = (
-                (first + second).astype(jnp.bfloat16).reshape(16, ROWS, size)
-            )
-            mixed[c, :, :, half + at : half + at + size] = (
-                (first - second).astype(jnp.bfloat16).reshape(16, ROWS, size)
-            )
+            plus, minus = (first + second).astype(jnp.bfloat16), (first - second).astype(jnp.bfloat16)
+            for i, e in enumerate(places):
+                here = slice(i * ROWS, (i + 1) * ROWS)
+                mixed[c, e, :, at : at + size] = plus[here]
+                mixed[c, e, :, half + at : half + at + size] = minus[here]
 
     def exchange(c, stages, source, target, send, recv):
         for offset in sum((OFFSETS[stage] for stage in stages), ()):
@@ -302,18 +302,10 @@
             ]
         interleave(flows)
 
-    def out_copy(g):
-        c, p, h = order[g]
-        at = (h * PIECES + p) * WIDE
-        return pltpu.make_async_copy(
-            result.at[g],
-            o_hbm.at[pl.ds(c * ROWS, ROWS), pl.ds(at, WIDE)],
-            out_sem.at[g],
-        )
-
     def finish(k):
         for h in range(2):
             g = 2 * k + h
+            c, p, _ = order[g]
             u, v, first, second = axes(h)
             count = 3 if k in DIRECT else 2
             landed = near2.at[g, pl.ds(0, count)]
@@ -321,20 +313,22 @@
             total = summed[g, v].astype(jnp.float32)
             for j in range(count):
                 total = total + near2[g, j].astype(jnp.float32)
-            result[g] = total.astype(jnp.bfloat16)
-            out_copy(g).start()
+            at = (h * PIECES + p) * WIDE
+            out[c * ROWS : (c + 1) * ROWS, at : at + WIDE] = total.astype(jnp.bfloat16)
 
     hear(0)
     table_load.wait()
     loads[0].wait()
-    rotate(0)
     for stage in range(4):
+        if stage < 2:
+            rotate(0, [partner(o) for o in OFFSETS[stage]])
+        if stage == 2:
+            rotate(0, [partner(o) for o in OFFSETS[2] + OFFSETS[3]] + [me])
         if stage > 0:
             hear(stage)
         exchange(0, (stage,), mixed, gathered, send_a, recv_a)
-        if stage == 1:
-            loads[1].wait()
-            rotate(1)
+    loads[1].wait()
+    rotate(1, list(range(16)))
     exchange(1, range(4), mixed, gathered, send_a, recv_a)
     for load in w_loads:
         load.start()
@@ -370,7 +364,6 @@
     for g in range(len(order)):
         fake(part.at[g, pl.ds(0, 3)], part.at[g, pl.ds(0, 3)], send1.at[g], recv_far.at[g]).wait_send()
         fake(summed.at[g, pl.ds(0, 3)], summed.at[g, pl.ds(0, 3)], send2.at[g], recv_far2.at[g]).wait_send()
-        out_copy(g).wait()
 
 
 def shards(activations, down_weight):
@@ -380,12 +373,11 @@
     bf16, f32 = jnp.bfloat16, jnp.float32
     groups = CHUNKS * PIECES * 2
     dma = pltpu.SemaphoreType.DMA
-    any_space = pl.BlockSpec(memory_space=pl.ANY)
     return pl.pallas_call(
         kernel,
         out_shape=jax.ShapeDtypeStruct((count_rows // 16, features), bf16),
-        in_specs=[any_space] * 3,
-        out_specs=any_space,
+        in_specs=[pl.BlockSpec(memory_space=pltpu.HBM)] * 3,
+        out_specs=pl.BlockSpec(memory_space=pltpu.VMEM),
         scratch_shapes=[
             pltpu.VMEM((CHUNKS, 16, ROWS, width), bf16),
             pltpu.VMEM(table.shape, bf16),
@@ -401,17 +393,15 @@
             pltpu.VMEM((groups, 4, ROWS, WIDE), bf16),
             pltpu.VMEM((groups, 2, ROWS, WIDE // 2), bf16),
             pltpu.VMEM((groups, 3, ROWS, WIDE), bf16),
-            pltpu.VMEM((groups, ROWS, WIDE), bf16),
             dma((CHUNKS + 1,)),
             dma((2 * PIECES,)),
             dma((CHUNKS,)), dma((CHUNKS,)), dma((CHUNKS,)), dma((CHUNKS,)),
             dma((groups,)), dma((groups,)),
             dma((groups,)), dma((groups,)), dma((groups,)), dma((groups,)),
-            dma((groups,)),
             pltpu.SemaphoreType.REGULAR((3,)),
         ],
         compiler_params=pltpu.CompilerParams(
-            collective_id=0, has_side_effects=True, vmem_limit_bytes=62 * 2**20
+            collective_id=0, has_side_effects=True, vmem_limit_bytes=53 * 2**20
         ),
         name="rotate_quantize_project",
     )(activations.reshape(16, count_rows // 16, width), table, down_weight)

time: 84.5 us -> 82.5 us (0.976)
  local copies, waits for them, and re-layouts: 1.77 us -> 0.75 us
  Pallas kernels: 82.6 us -> 81.6 us
    unnamed x1, local copies, waits for them, and re-layouts: 1.77 us -> 0.75 us
    pallas_call x1, Pallas kernels: 82.6 us -> 81.6 us  [shards(): pl.pallas_call(kernel, out_shape=jax.ShapeDtypeStruct((count_rows // 16,...]
where the time goes in v4:
time: 82.5 us; the launch traced here: 82.4 us
  Pallas kernels  81.6 us (99%)
    pallas_call x1, Pallas kernels, shards(): pl.pallas_call(kernel, out_shape=jax.ShapeDtypeStruct((count_rows // 16,...  81.6 us

profile of v4, /device:TPU:0, one launch (start us, length us, event | category | flops | bytes accessed | tf_op | source)
XLA Modules:
  0.0 82.4 jit_solution(15916797352922872638)
XLA Ops:
  0.0 81.6 %rotate_quantize_project.1 = bf16[32,6144]{1,0:T(8,128)(2,1)S(1)} custom-call(bf16[16,32,1792]{2,1,0:T(8,128)(2,1)} %bitcast.1, bf16[896,896]{1,0:T(8,128)(2,1)} %constant.2.clone.r_hbm, bf16[1792,6144]{1,0:T(8,128)(2,1)} %w_hbm.1), custom_call_target="tpu_custom_call" | custom-call | tf_op jit(solution)/shard_map/rotate_quantize_project/pallas_call | solution.py:376
  81.6 0.7 copy.5

commit v5 on v4

--- a/solution.py
+++ b/solution.py
@@ -349,12 +349,14 @@
     for g in range(each):
         relay(each + g)
         gather(g)
-    for g in range(each):
-        relay2(g)
-        gather(each + g)
+    relay2(0)
+    gather(each)
+    relay2(1)
+    gather(each + 1)
+    gather(each + 2)
+    relay2(2)
     for g in range(each):
         finish(g)
-        relay2(each + g)
     for g in range(each):
         finish(each + g)
 

time: 82.5 us -> 82.6 us (level)
  no operation moved by 1% of the time
where the time goes in v5:
time: 82.6 us; the launch traced here: 82.2 us
  Pallas kernels  81.4 us (99%)
    pallas_call x1, Pallas kernels, shards(): pl.pallas_call(kernel, out_shape=jax.ShapeDtypeStruct((count_rows // 16,...  81.4 us

profile of v5, /device:TPU:0, one launch (start us, length us, event | category | flops | bytes accessed | tf_op | source)
XLA Modules:
  0.0 82.2 jit_solution(567346780430858908)
XLA Ops:
  0.0 81.4 %rotate_quantize_project.1 = bf16[32,6144]{1,0:T(8,128)(2,1)S(1)} custom-call(bf16[16,32,1792]{2,1,0:T(8,128)(2,1)} %bitcast.1, bf16[896,896]{1,0:T(8,128)(2,1)} %constant.2.clone.r_hbm, bf16[1792,6144]{1,0:T(8,128)(2,1)} %w_hbm.1), custom_call_target="tpu_custom_call" | custom-call | tf_op jit(solution)/shard_map/rotate_quantize_project/pallas_call | solution.py:378
  81.4 0.7 copy.5

commit v6 on v4

--- a/solution.py
+++ b/solution.py
@@ -14,7 +14,7 @@
 ROWS = 16
 PIECES = 3
 WIDE = 1024
-DIRECT = (3, 4, 5)
+DIRECT = (2, 3, 4, 5)
 OFFSETS = (
     ((0, 1), (1, 0), (0, 3), (3, 0)),
     ((1, 1), (3, 3), (1, 3), (3, 1), (0, 2), (2, 0)),

time: 82.5 us -> 82.8 us (level)
  no operation moved by 1% of the time
where the time goes in v6:
time: 82.8 us; the launch traced here: 82.5 us
  Pallas kernels  81.7 us (99%)
    pallas_call x1, Pallas kernels, shards(): pl.pallas_call(kernel, out_shape=jax.ShapeDtypeStruct((count_rows // 16,...  81.7 us

profile of v6, /device:TPU:0, one launch (start us, length us, event | category | flops | bytes accessed | tf_op | source)
XLA Modules:
  0.0 82.5 jit_solution(14488335219026715669)
XLA Ops:
  0.0 81.7 %rotate_quantize_project.1 = bf16[32,6144]{1,0:T(8,128)(2,1)S(1)} custom-call(bf16[16,32,1792]{2,1,0:T(8,128)(2,1)} %bitcast.1, bf16[896,896]{1,0:T(8,128)(2,1)} %constant.2.clone.r_hbm, bf16[1792,6144]{1,0:T(8,128)(2,1)} %w_hbm.1), custom_call_target="tpu_custom_call" | custom-call | tf_op jit(solution)/shard_map/rotate_quantize_project/pallas_call | solution.py:376
  81.7 0.7 copy.5
